TPU v7x, 32 devices: a whole 2x2x4 slice. The times are simulated.
32 devices in a mesh: gx: 4 (over y, core), gy: 8 (over z, x).
Axes of the slice: x: 2, y: 2, z: 4, core: 2. Of those that a mesh axis runs over, the one named last changes fastest.
Arguments:
- wavefield: float32 [8, 16, 3, 125, 256], P('gx', 'gy'), may hold values from -0.6 to 0.6
- moduli: float32 [8, 16, 2, 256], P('gx', 'gy'), may hold values from 0.5 to 4
- residuals: float32 [32, 32, 128], P(('gx', 'gy')), may hold values from -6 to 6
- coords: float32 [32, 32, 3, 128], P(('gx', 'gy')), may hold values from -1 to 1
- angles: float32 [32, 32, 2, 128], P(('gx', 'gy')), may hold values from -3.140625 to 3.140625
- element_ids: int32 [32, 32, 128], P(('gx', 'gy')), may hold values from 0 to 1023
- counts: int32 [32, 32], P(('gx', 'gy')), may hold values from 0 to 128, as said below
Outputs:
- force: float32 [8, 16, 3, 125, 256], P('gx', 'gy')
Inputs may be any that keep to these rules, and one draw needn't show every extreme that they name: `counts`: each sending device has at least one tile with exactly 128 live slots; in every draw one owner receives 128 live slots from every sender. The lightest owners receive on average about a sixth of 128 a sender, the others lie between.
All inputs are finite; a program needn't handle non-finite values.
Results may differ from a plain program's by a relative error of at most 0.0003.
Values sent between devices are 32-bit elements; how exact they have to be, the bound alone decides.
A program may use at most 64 MiB of HBM per device.

v0:
```python
import functools
import math

import jax
import jax.numpy as jnp
import numpy as np
from jax import lax
from jax.experimental import pallas as pl
from jax.experimental.pallas import tpu as pltpu
from jax.sharding import PartitionSpec as P

MESH = pl.DeviceIdType.MESH
F32, BF16 = jnp.float32, jnp.bfloat16
PAD = 128
SPAN = 32


def gll_points():
    return np.array([-1.0, -math.sqrt(3.0 / 7.0), 0.0, math.sqrt(3.0 / 7.0), 1.0])


def gll_weights():
    return np.array([0.1, 49.0 / 90.0, 32.0 / 45.0, 49.0 / 90.0, 0.1])


def derivative_table():
    points = gll_points()
    table = np.zeros((5, 5))
    for row in range(5):
        for col in range(5):
            if row == col:
                table[row, col] = sum(
                    (1.0 / (points[col] - points[other]) for other in range(5) if other != col)
                )
            else:
                value = 1.0 / (points[col] - points[row])
                for other in range(5):
                    if other != col and other != row:
                        value = (
                            value * (points[row] - points[other]) / (points[col] - points[other])
                        )
                table[row, col] = value
    return table


def split_table(table):
    high = table.astype(BF16)
    return high, (table - high.astype(np.float64)).astype(BF16)


def tables():
    dm, eye = derivative_table(), np.eye(5)
    w1 = gll_weights()
    weight = (w1[:, None, None] * w1[None, :, None] * w1[None, None, :]).reshape(-1)
    dirs = [
        np.kron(np.kron(dm, eye), eye),
        np.kron(np.kron(eye, dm), eye),
        np.kron(np.kron(eye, eye), dm),
    ]
    grad = np.zeros((3 * PAD, PAD))
    back = np.zeros((PAD, 3 * PAD))
    for j in range(3):
        grad[j * PAD : j * PAD + 125, :125] = dirs[j]
        back[:125, j * PAD : j * PAD + 125] = -dirs[j].T * weight[None, :]
    gh, gl = split_table(grad)
    bh, bl = split_table(back)
    g1 = np.concatenate([gh, gh], 1)
    bs = np.concatenate([bh, bl], 0)
    spread = np.zeros((4 * PAD, 192))
    for p in range(5):
        for q in range(5):
            for r in range(5):
                n = (p * 5 + q) * 5 + r
                for base, col in ((0, p * 8 + q), (1, 40 + p * 8 + q), (2, 80 + r), (3, 88 + r)):
                    spread[base * PAD + n, col] = 1.0
                    spread[base * PAD + n, 96 + col] = 1.0
    points = gll_points()
    consts = np.zeros((8, 8, 128), np.float32)
    for q in range(5):
        others = [k for k in range(5) if k != q]
        for j, k in enumerate(others):
            consts[j, q] = points[k]
            consts[4 + j, q] = 1.0 / (points[q] - points[k])
    return (
        jnp.asarray(g1),
        jnp.asarray(gl),
        jnp.asarray(bs),
        jnp.asarray(spread.astype(BF16)),
        jnp.asarray(consts),
    )


def split(x):
    high = x.astype(BF16)
    return high, (x - high.astype(F32)).astype(BF16)


def dot(a, b):
    return jnp.dot(a, b, preferred_element_type=F32)


def dot_t(a, b):
    return lax.dot_general(a, b, (((1,), (1,)), ((), ())), preferred_element_type=F32)


def basis(row, const):
    x = jnp.broadcast_to(row, const[0].shape)
    value = slope = None
    for j in range(4):
        scale = const[4 + j]
        factor = (x - const[j]) * scale
        if value is None:
            value, slope = factor, scale
        else:
            slope = slope * factor + value * scale
            value = value * factor
    return value, slope


def step_kernel(
    nx, ny, cx, cy, resid, coord, angle, ids, count, u_ref, mod_ref, g1, g2, bs, spread, consts,
    out, packed, got, acc, lhs, hot, pad, xs, ys, cs, rx, ry, rc,
    send_sem, recv_sem, halo_send, halo_recv,
):
    n = nx * ny
    gx, gy = lax.axis_index("gx"), lax.axis_index("gy")
    me = gx * ny + gy
    cells, depth, slots = cx * cy, acc.shape[2], resid.shape[2]
    halves = depth // 128
    rows_node = halves * cy
    span = min(n, SPAN)
    width = 2 * slots
    barrier = pltpu.get_barrier_semaphore()

    def greet(k, c):
        to = lax.rem(me + k, n)
        pl.semaphore_signal(
            barrier, inc=1, device_id=(to // ny, lax.rem(to, ny)), device_id_type=MESH
        )
        return c

    lax.fori_loop(1, n, greet, 0)
    rows = lax.broadcasted_iota(jnp.int32, (n, n), 0)
    cols = lax.broadcasted_iota(jnp.int32, (n, n), 1)
    diagonal = jnp.where(rows == cols, count[...].astype(F32), 0.0)
    live_count = jnp.sum(diagonal, axis=1, keepdims=True)
    slot = lax.broadcasted_iota(jnp.int32, (n, slots), 1).astype(F32)
    az, dip = angle[0, :, 0, :], angle[0, :, 1, :]
    cd = jnp.cos(dip)
    packed[:, 0, :] = jnp.where(slot < live_count, resid[0], 0.0)
    for d in range(3):
        packed[:, 1 + d, :] = coord[0, d]
    packed[:, 4, :] = jnp.cos(az) * cd
    packed[:, 5, :] = jnp.sin(az) * cd
    packed[:, 6, :] = jnp.sin(dip)
    packed[:, 7, :] = ids[0].astype(F32)
    pl.semaphore_wait(barrier, n - 1)

    def tile_copy(k, to, at):
        return pltpu.make_async_remote_copy(
            src_ref=packed.at[to],
            dst_ref=got.at[at],
            send_sem=send_sem.at[k],
            recv_sem=recv_sem.at[k],
            device_id=(to // ny, lax.rem(to, ny)),
            device_id_type=MESH,
        )

    def send(k, c):
        tile_copy(k, lax.rem(me + k, n), me).start()
        return c

    lax.fori_loop(1, n, send, 0)
    got[me] = packed[me]

    pad[...] = jnp.zeros_like(pad)

    def stiff(cell, carry):
        g = []
        for c in range(3):
            start = ((cell // cy) * 3 + c) * 125 * rows_node + lax.rem(cell, cy)
            for h in range(halves):
                pad[0:125, h * 128 : (h + 1) * 128] = u_ref[
                    pl.ds(start + h * cy, 125, stride=rows_node), :
                ]
            high, low = split(pad[...])
            r = dot(g1[...], jnp.concatenate([high, low], axis=0)) + dot(g2[...], high)
            g.append([r[j * PAD : (j + 1) * PAD] for j in range(3)])
        lam, mu = mod_ref[cell, 0:1, :], mod_ref[cell, 1:2, :]
        press = lam * (g[0][0] + g[1][1] + g[2][2])
        for i in range(3):
            parts = []
            for j in range(3):
                s = mu * (g[i][j] + g[j][i])
                parts.append(s + press if i == j else s)
            high, low = split(jnp.concatenate(parts, axis=0))
            r = dot(bs[...], high)
            acc[cell, i * PAD : (i + 1) * PAD, :] = r[:PAD] + r[PAD:] + dot(bs[:PAD], low)
        return carry

    lax.fori_loop(0, cells, stiff, 0)

    def arrive(k, c):
        tile_copy(k, lax.rem(me + k, n), lax.rem(me - k + n, n)).wait_recv()
        return c

    lax.fori_loop(1, n, arrive, 0)

    def prepare(first_tile):
        def pair(k, carry):
            at = first_tile + 2 * k
            tile = jnp.concatenate([got[at], got[at + 1]], axis=1)
            const = [jnp.concatenate([consts[j], consts[j]], axis=1) for j in range(8)]
            v = tile[0:1]
            t = [tile[4 + i : 5 + i] for i in range(3)]
            lx, dx = basis(tile[1:2], const)
            ly, dy = basis(tile[2:3], const)
            lz, dz = basis(tile[3:4], const)
            dx, dy, dz = dx * t[0], dy * t[1], dz * t[2]
            first = [dx[p : p + 1] * ly + lx[p : p + 1] * dy for p in range(5)]
            second = [lx[p : p + 1] * ly for p in range(5)]
            high, low = split(jnp.concatenate(first + second + [lz, dz], axis=0))
            wide = dot(spread[...], jnp.concatenate([high, low], axis=0))
            shape = wide[:PAD] * wide[2 * PAD : 3 * PAD] + wide[PAD : 2 * PAD] * wide[3 * PAD :]
            cols = pl.ds(pl.multiple_of(k * width, width), width)
            for i in range(3):
                high, low = split(shape * (v * t[i]))
                lhs[i, :PAD, cols] = high
                lhs[i, PAD:, cols] = low
            ident = tile[7:8].astype(jnp.int32)
            number = lax.broadcasted_iota(jnp.int32, (cells * depth, width), 0)
            hot[:, cols] = jnp.where(number == ident, 1.0, 0.0).astype(BF16)
            return carry

        lax.fori_loop(0, span // 2, pair, 0)

    def gather(i, cell):
        r = dot_t(lhs[i], hot[cell * depth : (cell + 1) * depth, :])
        return acc[cell, i * PAD : (i + 1) * PAD, :] + r[:PAD] + r[PAD:]

    if n > span:
        def early(b, carry):
            prepare(b * span)
            for i in range(3):
                for cell in range(cells):
                    acc[cell, i * PAD : (i + 1) * PAD, :] = gather(i, cell)
            return carry

        lax.fori_loop(0, n // span - 1, early, 0)
    prepare(n - span)

    node = lax.broadcasted_iota(jnp.int32, (PAD, depth), 0)
    lane = lax.broadcasted_iota(jnp.int32, (PAD, depth), 1)
    along = lax.rem(node, 5)
    take_up = (along == 4) & (lane < depth - 1)
    take_down = (along == 0) & (lane > 0)

    def join(a, ra, b, rb, size):
        total = acc[a, ra : ra + size, :] + acc[b, rb : rb + size, :]
        acc[a, ra : ra + size, :] = total
        acc[b, rb : rb + size, :] = total

    moves = []
    for side in (0, 1):
        moves.append((2 * side - 1, 0, xs, rx, (side,), (1 - side,)))
    for side in (0, 1):
        moves.append((0, 2 * side - 1, ys, ry, (side,), (1 - side,)))
    for x in (0, 1):
        for y in (0, 1):
            moves.append((2 * x - 1, 2 * y - 1, cs, rc, (x, y), (1 - x, 1 - y)))
    opposite = [1, 0, 3, 2, 7, 6, 5, 4]

    def there(m):
        ok = None
        for pos, step, total in ((gx, moves[m][0], nx), (gy, moves[m][1], ny)):
            if step:
                c = pos > 0 if step < 0 else pos < total - 1
                ok = c if ok is None else ok & c
        return ok

    def strip_copy(c, m, sem, place):
        dx, dy, src, dst, mine, theirs = moves[m]
        return pltpu.make_async_remote_copy(
            src_ref=src.at[(c,) + mine],
            dst_ref=dst.at[(c,) + place],
            send_sem=halo_send.at[c * 8 + m],
            recv_sem=halo_recv.at[c * 8 + sem],
            device_id=(gx + dx, gy + dy),
            device_id_type=MESH,
        )

    for m in range(8):
        @pl.when(jnp.logical_not(there(m)))
        def _():
            dst, mine = moves[m][3], moves[m][4]
            for c in range(3):
                hole = dst.at[(c,) + mine]
                hole[...] = jnp.zeros(hole.shape, F32)

    for c in range(3):
        o = c * PAD
        for cell in range(cells):
            f = gather(c, cell)
            up = pltpu.roll(pltpu.roll(f, depth - 1, 1), 4, 0)
            down = pltpu.roll(pltpu.roll(f, 1, 1), PAD - 4, 0)
            acc[cell, o : o + PAD, :] = (
                f + jnp.where(take_up, up, 0.0) + jnp.where(take_down, down, 0.0)
            )
        for y in range(cy):
            for x in range(cx - 1):
                join(x * cy + y, o + 100, (x + 1) * cy + y, o, 25)
        for x in range(cx):
            for y in range(cy - 1):
                for p in range(5):
                    join(x * cy + y, o + p * 25 + 20, x * cy + y + 1, o + p * 25, 5)
        for y in range(cy):
            xs[c, 0, y] = acc[y, o : o + 25, :]
            xs[c, 1, y] = acc[(cx - 1) * cy + y, o + 100 : o + 125, :]
        for x in range(cx):
            for p in range(5):
                k = o + p * 25
                ys[c, 0, x, p * 5 : p * 5 + 5, :] = acc[x * cy, k : k + 5, :]
                ys[c, 1, x, p * 5 : p * 5 + 5, :] = acc[x * cy + cy - 1, k + 20 : k + 25, :]
        for x in range(2):
            for y in range(2):
                cell = x * (cx - 1) * cy + y * (cy - 1)
                k = o + x * 100 + y * 20
                cs[c, x, y] = acc[cell, k : k + 5, :]
        for m in range(8):
            @pl.when(there(m))
            def _():
                strip_copy(c, m, m, moves[m][5]).start()

    def drain(k, c):
        tile_copy(k, lax.rem(me + k, n), me).wait_send()
        return c

    lax.fori_loop(1, n, drain, 0)

    for c in range(3):
        o = c * PAD
        for m in range(8):
            @pl.when(there(m))
            def _():
                strip_copy(c, m, opposite[m], moves[m][4]).wait_recv()
                strip_copy(c, m, m, moves[m][5]).wait_send()

        for y in range(cy):
            acc[y, o : o + 25, :] += rx[c, 0, y]
            acc[(cx - 1) * cy + y, o + 100 : o + 125, :] += rx[c, 1, y]
        for x in range(cx):
            for p in range(5):
                k = o + p * 25
                acc[x * cy, k : k + 5, :] += ry[c, 0, x, p * 5 : p * 5 + 5, :]
                acc[x * cy + cy - 1, k + 20 : k + 25, :] += ry[c, 1, x, p * 5 : p * 5 + 5, :]
        for x in range(2):
            for y in range(2):
                cell = x * (cx - 1) * cy + y * (cy - 1)
                k = o + x * 100 + y * 20
                acc[cell, k : k + 5, :] += rc[c, x, y]
        for cell in range(cells):
            start = ((cell // cy) * 3 + c) * 125 * rows_node + cell % cy
            for h in range(halves):
                out[pl.ds(start + h * cy, 125, stride=rows_node), :] = acc[
                    cell, o : o + 125, h * 128 : (h + 1) * 128
                ]


def vmem(count):
    return [pl.BlockSpec(memory_space=pltpu.VMEM)] * count


def body(nx, ny, wavefield, moduli, residuals, coords, angles, element_ids, counts):
    cx, cy, depth = wavefield.shape[0], wavefield.shape[1], wavefield.shape[4]
    n, slots = nx * ny, residuals.shape[2]
    cells, halves = cx * cy, depth // 128
    span = min(n, SPAN)
    rows = wavefield.transpose(0, 2, 3, 1, 4).reshape(cx, 3, 125, cy, halves, 128)
    rows = rows.transpose(0, 1, 2, 4, 3, 5).reshape(-1, 128)
    scratch = [
        pltpu.VMEM((n, 8, slots), F32),
        pltpu.VMEM((n, 8, slots), F32),
        pltpu.VMEM((cells, 3 * PAD, depth), F32),
        pltpu.VMEM((3, 2 * PAD, span * slots), BF16),
        pltpu.VMEM((cells * depth, span * slots), BF16),
        pltpu.VMEM((PAD, depth), F32),
    ]
    for _ in range(2):
        scratch += [
            pltpu.VMEM((3, 2, cy, 25, depth), F32),
            pltpu.VMEM((3, 2, cx, 25, depth), F32),
            pltpu.VMEM((3, 2, 2, 5, depth), F32),
        ]
    scratch += [
        pltpu.SemaphoreType.DMA((n,)),
        pltpu.SemaphoreType.DMA((n,)),
        pltpu.SemaphoreType.DMA((24,)),
        pltpu.SemaphoreType.DMA((24,)),
    ]
    force = pl.pallas_call(
        functools.partial(step_kernel, nx, ny, cx, cy),
        out_shape=jax.ShapeDtypeStruct(rows.shape, F32),
        in_specs=vmem(12),
        out_specs=vmem(1)[0],
        scratch_shapes=scratch,
        compiler_params=pltpu.CompilerParams(collective_id=0, has_side_effects=True),
    )(
        residuals,
        coords.transpose(0, 2, 1, 3),
        angles,
        element_ids,
        counts,
        rows,
        moduli.reshape(cells, 2, depth),
        *tables(),
    )
    force = force.reshape(cx, 3, 125, halves, cy, 128).transpose(0, 1, 2, 4, 3, 5)
    return force.reshape(cx, 3, 125, cy, depth).transpose(0, 3, 1, 2, 4)


def solution(mesh):
    in_specs = (
        P("gx", "gy", None, None, None),
        P("gx", "gy", None, None),
        P(("gx", "gy"), None, None),
        P(("gx", "gy"), None, None, None),
        P(("gx", "gy"), None, None, None),
        P(("gx", "gy"), None, None),
        P(("gx", "gy"), None),
    )
    out_specs = P("gx", "gy", None, None, None)
    return jax.shard_map(
        functools.partial(body, mesh.shape["gx"], mesh.shape["gy"]),
        mesh=mesh,
        in_specs=in_specs,
        out_specs=out_specs,
        check_vma=False,
    )
```

profile of v0, /device:TPU:0, one launch (start us, length us, event | category | flops | bytes accessed | tf_op | source)
XLA Modules:
  0.0 42.0 jit_solution(3110975555915151102)
XLA Ops:
  0.0 39.0 %shard_map.118 = f32[3000,128]{1,0:T(8,128)} custom-call(f32[1,32,128]{2,1,0:T(8,128)} %resid.1, f32[1,3,32,128]{3,2,1,0:T(8,128)} %bitcast.18, f32[1,32,2,128]{3,2,1,0:T(2,128)} %angle.1, s32[1,32,128]{2,1,0:T(8,128)} %ids.1, s32[1,32]{1,0:T(1,128)} %count.1, f32[3000,128]{1,0:T(8,128)} %bitcast.17, f32[4,2,256]{2,1,0:T(2,128)} %bitcast.19, ...), custom_call_target="tpu_custom_call" | custom-call | tf_op jit(solution)/shard_map/pallas_call | solution.py:400
  39.0 3.1 %copy.15 = f32[2,2,3,125,256]{4,1,3,2,0:T(2,128)} copy(f32[2,2,3,125,256]{4,1,3,2,0:T(2,128)} %bitcast.16) | data formatting | bytes 3072000
where the time goes:
time: 42.2 us; the launch traced here: 42 us
  Pallas kernels  39 us (92%)
  local copies, waits for them, and re-layouts  3.05 us (7%)
    pallas_call x1, Pallas kernels, body(): pl.pallas_call(functools.partial(step_kernel, nx, ny, cx, cy), out_shape=...  39 us
    unnamed x1, local copies, waits for them, and re-layouts  3.05 us

commit v1 on v0

v1 whole, which is shorter than its diff:
```python
import functools
import math

import jax
import jax.numpy as jnp
import numpy as np
from jax import lax
from jax.experimental import pallas as pl
from jax.experimental.pallas import tpu as pltpu
from jax.sharding import PartitionSpec as P

MESH = pl.DeviceIdType.MESH
F32, BF16 = jnp.float32, jnp.bfloat16
PAD = 128
SPAN = 32
TILES = 4
RING, CORE = 80, 48

EDGE = [(0, 0), (0, 1), (0, 2), (0, 3), (0, 4), (1, 0), (2, 0), (3, 0)]
EDGE += [(4, 0), (4, 1), (4, 2), (4, 3), (4, 4), (1, 4), (2, 4), (3, 4)]
INNER = [(1, 1), (1, 2), (1, 3), (2, 1), (2, 2), (2, 3), (3, 1), (3, 2)]
LAST = (3, 3)


def node_order():
    order = []
    for r in range(5):
        order += [(p * 5 + q) * 5 + r for p, q in EDGE]
    for r in range(5):
        order += [(p * 5 + q) * 5 + r for p, q in INNER]
    order += [(LAST[0] * 5 + LAST[1]) * 5 + r for r in range(5)]
    return np.array(order)


def gll_points():
    return np.array([-1.0, -math.sqrt(3.0 / 7.0), 0.0, math.sqrt(3.0 / 7.0), 1.0])


def gll_weights():
    return np.array([0.1, 49.0 / 90.0, 32.0 / 45.0, 49.0 / 90.0, 0.1])


def derivative_table():
    points = gll_points()
    table = np.zeros((5, 5))
    for row in range(5):
        for col in range(5):
            if row == col:
                table[row, col] = sum(
                    (1.0 / (points[col] - points[other]) for other in range(5) if other != col)
                )
            else:
                value = 1.0 / (points[col] - points[row])
                for other in range(5):
                    if other != col and other != row:
                        value = (
                            value * (points[row] - points[other]) / (points[col] - points[other])
                        )
                table[row, col] = value
    return table


def split_table(table):
    high = table.astype(BF16)
    return high, (table - high.astype(np.float64)).astype(BF16)


def roots(k):
    points = gll_points()
    others = [m for m in range(5) if m != k]
    return [points[m] for m in others], 1.0 / np.prod([points[k] - points[m] for m in others])


def tables():
    dm, eye = derivative_table(), np.eye(5)
    w1 = gll_weights()
    weight = (w1[:, None, None] * w1[None, :, None] * w1[None, None, :]).reshape(-1)
    dirs = [
        np.kron(np.kron(dm, eye), eye),
        np.kron(np.kron(eye, dm), eye),
        np.kron(np.kron(eye, eye), dm),
    ]
    order = node_order()
    grad = np.zeros((3 * PAD, PAD))
    back = np.zeros((PAD, 3 * PAD))
    for j in range(3):
        grad[j * PAD : j * PAD + 125, :125] = dirs[j][order]
        full = -dirs[j].T * weight[None, :]
        back[:125, j * PAD : j * PAD + 125] = full[order][:, order]
    gh, gl = split_table(grad)
    bh, bl = split_table(back)
    g1 = np.concatenate([gh, gh], 1)
    bs = np.concatenate([bh, bl], 0)
    consts = np.zeros((41, 8, 128), np.float32)
    for g, group in enumerate((EDGE[:8], EDGE[8:], INNER, [LAST] * 8)):
        for row, (p, q) in enumerate(group):
            rp, sp = roots(p)
            rq, sq = roots(q)
            for j in range(4):
                consts[g * 9 + j, row] = rp[j]
                consts[g * 9 + 4 + j, row] = rq[j]
            consts[g * 9 + 8, row] = sp * sq
    for r in range(5):
        rr, sr = roots(r)
        for j in range(4):
            consts[36 + j, r] = rr[j]
        consts[40, r] = sr
    return jnp.asarray(g1), jnp.asarray(gl), jnp.asarray(bs), jnp.asarray(consts)


def split(x):
    high = x.astype(BF16)
    return high, (x - high.astype(F32)).astype(BF16)


def dot(a, b):
    return jnp.dot(a, b, preferred_element_type=F32)


def sin_cos(x):
    h = x * 0.5
    h2 = h * h
    s = c = None
    for k in range(6, -1, -1):
        a = (-1.0) ** k / math.factorial(2 * k + 1)
        b = (-1.0) ** k / math.factorial(2 * k)
        s = jnp.full(x.shape, a, F32) if s is None else s * h2 + a
        c = jnp.full(x.shape, b, F32) if c is None else c * h2 + b
    s = s * h
    return 2.0 * s * c, 1.0 - 2.0 * s * s


def quartic(x, rows):
    a, b, c, d = [x - row for row in rows]
    ab, cd = a * b, c * d
    return ab * cd, (a + b) * cd + ab * (c + d)


def moves_of(cx, cy):
    moves = [(2 * s - 1, 0) for s in (0, 1)] + [(0, 2 * s - 1) for s in (0, 1)]
    moves += [(2 * x - 1, 2 * y - 1) for x in (0, 1) for y in (0, 1)]
    return moves


OPPOSITE = [1, 0, 3, 2, 7, 6, 5, 4]


def neighbour(m, gx, gy, nx, ny, cx, cy):
    ok = None
    for pos, step, total in ((gx, moves_of(cx, cy)[m][0], nx), (gy, moves_of(cx, cy)[m][1], ny)):
        if step:
            c = pos > 0 if step < 0 else pos < total - 1
            ok = c if ok is None else ok & c
    return ok


def step_kernel(
    nx, ny, cx, cy, resid_h, coord_h, angle_h, ids_h, count_h, u_h, mod_h, g1_h, g2_h, bs_h,
    consts_h, pre_h, rx, ry, rc,
    resid, coord, angle, ids, count, u_ref, mod_ref, g1, g2, bs, consts, pre,
    packed, got, acc, lhs_a, lhs_b, in_a, in_b, hot_a, hot_b, pad, xs, ys, cs,
    load_sem, store_sem, send_sem, recv_sem, halo_send, halo_recv,
):
    n = nx * ny
    gx, gy = lax.axis_index("gx"), lax.axis_index("gy")
    me = gx * ny + gy
    cells, depth, slots = cx * cy, acc.shape[2], resid.shape[2]
    halves = depth // 128
    rows_node = halves * cy
    span = min(n, SPAN)
    chunks = span // TILES
    width = TILES * slots
    barrier = pltpu.get_barrier_semaphore()

    def greet(k, c):
        to = lax.rem(me + k, n)
        pl.semaphore_signal(
            barrier, inc=1, device_id=(to // ny, lax.rem(to, ny)), device_id_type=MESH
        )
        return c

    pairs = [
        (count_h, count), (angle_h, angle), (resid_h, resid), (coord_h, coord), (ids_h, ids),
        (u_h, u_ref), (mod_h, mod_ref), (g1_h, g1), (g2_h, g2), (bs_h, bs), (consts_h, consts),
    ]
    loads = [pltpu.make_async_copy(a, b, load_sem.at[k]) for k, (a, b) in enumerate(pairs)]
    for copy in loads:
        copy.start()
    lax.fori_loop(1, n, greet, 0)
    for copy in loads[:5]:
        copy.wait()

    rows = lax.broadcasted_iota(jnp.int32, (n, n), 0)
    cols = lax.broadcasted_iota(jnp.int32, (n, n), 1)
    diagonal = jnp.where(rows == cols, count[...].astype(F32), 0.0)
    live_count = jnp.sum(diagonal, axis=1, keepdims=True)
    slot = lax.broadcasted_iota(jnp.int32, (n, slots), 1).astype(F32)
    sa, ca = sin_cos(angle[0, :, 0, :])
    sd, cd = sin_cos(angle[0, :, 1, :])
    packed[:, 0, :] = jnp.where(slot < live_count, resid[0], 0.0)
    for d in range(3):
        packed[:, 1 + d, :] = coord[0, d]
    packed[:, 4, :] = ca * cd
    packed[:, 5, :] = sa * cd
    packed[:, 6, :] = sd
    packed[:, 7, :] = ids[0].astype(F32)
    pl.semaphore_wait(barrier, n - 1)

    def tile_copy(k, to, at):
        return pltpu.make_async_remote_copy(
            src_ref=packed.at[to],
            dst_ref=got.at[at],
            send_sem=send_sem.at[k],
            recv_sem=recv_sem.at[k],
            device_id=(to // ny, lax.rem(to, ny)),
            device_id_type=MESH,
        )

    def send(k, c):
        tile_copy(k, lax.rem(me + k, n), me).start()
        return c

    lax.fori_loop(1, n, send, 0)
    got[me] = packed[me]
    pad[...] = jnp.zeros_like(pad)
    for copy in loads[5:]:
        copy.wait()

    def stiff(cell, slab):
        g = []
        for c in range(3):
            start = ((cell // cy) * 3 + c) * 125 * rows_node + cell % cy
            for h in range(halves):
                pad[slab, c, 0:125, h * 128 : (h + 1) * 128] = u_ref[
                    pl.ds(start + h * cy, 125, stride=rows_node), :
                ]
            high, low = split(pad[slab, c])
            r = dot(g1[...], jnp.concatenate([high, low], axis=0)) + dot(g2[...], high)
            g.append([r[j * PAD : (j + 1) * PAD] for j in range(3)])
        lam, mu = mod_ref[cell, 0:1, :], mod_ref[cell, 1:2, :]
        press = lam * (g[0][0] + g[1][1] + g[2][2])
        for i in range(3):
            parts = []
            for j in range(3):
                s = mu * (g[i][j] + g[j][i])
                parts.append(s + press if i == j else s)
            high, low = split(jnp.concatenate(parts, axis=0))
            r = dot(bs[...], high)
            acc[cell, i * PAD : (i + 1) * PAD, :] = r[:PAD] + r[PAD:] + dot(bs[:PAD], low)

    for cell in range(cells):
        stiff(cell, cell % 2)

    def wait_tile(k):
        tile_copy(k, lax.rem(me + k, n), lax.rem(me - k + n, n)).wait_recv()

    def prepare(first, ring, inner, hot, at):
        tiles = [got[lax.rem(me - (first + i) + n, n)] for i in range(TILES)]
        tile = jnp.concatenate(tiles, axis=1)

        def const(k):
            return jnp.concatenate([consts[k]] * TILES, axis=1)

        v = tile[0:1]
        t = [tile[4 + i : 5 + i] for i in range(3)]
        x, y, z = [jnp.broadcast_to(tile[1 + d : 2 + d], (8, width)) for d in range(3)]
        lz, dz = quartic(z, [const(36 + j) for j in range(4)])
        lz, dz = lz * const(40), dz * (const(40) * t[2])
        first_of, second_of = [], []
        for g in range(4):
            lx, dx = quartic(x, [const(g * 9 + j) for j in range(4)])
            ly, dy = quartic(y, [const(g * 9 + 4 + j) for j in range(4)])
            scale = const(g * 9 + 8)
            first_of.append(scale * ((t[0] * dx) * ly + (t[1] * dy) * lx))
            second_of.append(scale * (lx * ly))
        edge, core = [], []
        for r in range(5):
            a = jnp.broadcast_to(lz[r : r + 1], (8, width))
            b = jnp.broadcast_to(dz[r : r + 1], (8, width))
            edge += [first_of[g] * a + second_of[g] * b for g in (0, 1)]
            core.append(first_of[2] * a + second_of[2] * b)
        core.append(first_of[3] * lz + second_of[3] * dz)
        edge, core = jnp.concatenate(edge, axis=0), jnp.concatenate(core, axis=0)
        for i in range(3):
            w = v * t[i]
            high, low = split(edge * w)
            ring[2 * i * RING : (2 * i + 1) * RING, :] = high
            ring[(2 * i + 1) * RING : (2 * i + 2) * RING, :] = low
            high, low = split(core * w)
            inner[2 * i * CORE : (2 * i + 1) * CORE, pl.ds(at, width)] = high
            inner[(2 * i + 1) * CORE : (2 * i + 2) * CORE, pl.ds(at, width)] = low
        number = lax.broadcasted_iota(jnp.int32, (slots, cells * depth), 1).astype(F32)
        for i in range(TILES):
            ident = tiles[i].T[:, 7:8]
            hot[pl.ds(at + i * slots, slots), :] = jnp.where(number == ident, 1.0, 0.0).astype(BF16)

    def gather_ring(ring, hot, at):
        for cell in range(cells):
            r = dot(ring[...], hot[pl.ds(at, width), cell * depth : (cell + 1) * depth])
            for i in range(3):
                acc[cell, i * PAD : i * PAD + RING, :] += (
                    r[2 * i * RING : (2 * i + 1) * RING]
                    + r[(2 * i + 1) * RING : (2 * i + 2) * RING]
                )

    def gather_core(cell):
        where = slice(cell * depth, (cell + 1) * depth)
        r = dot(in_a[...], hot_a[:, where]) + dot(in_b[...], hot_b[:, where])
        return [
            acc[cell, i * PAD + RING : (i + 1) * PAD, :]
            + r[2 * i * CORE : (2 * i + 1) * CORE]
            + r[(2 * i + 1) * CORE : (2 * i + 2) * CORE]
            for i in range(3)
        ]

    def inject(first, last):
        for i in range(TILES):
            wait_tile(first + i)
        prepare(first, lhs_a, in_a, hot_a, 0)

        def pair(j, carry):
            one, two = first + (2 * j + 1) * TILES, first + (2 * j + 2) * TILES
            for i in range(2 * TILES):
                wait_tile(one + i)
            here = pl.multiple_of(j * width, width)
            then = pl.multiple_of((j + 1) * width, width)
            prepare(one, lhs_b, in_b, hot_b, here)
            gather_ring(lhs_a, hot_a, here)
            prepare(two, lhs_a, in_a, hot_a, then)
            gather_ring(lhs_b, hot_b, here)
            return carry

        half = chunks // 2
        lax.fori_loop(0, half - 1, pair, 0)
        end = first + (chunks - 1) * TILES
        for i in range(TILES - 1 if last else TILES):
            wait_tile(end + i)
        prepare(end, lhs_b, in_b, hot_b, (half - 1) * width)
        gather_ring(lhs_a, hot_a, (half - 1) * width)
        gather_ring(lhs_b, hot_b, (half - 1) * width)

    if n > span:
        def early(b, carry):
            inject(b * span + 1, False)
            for cell in range(cells):
                for i, f in enumerate(gather_core(cell)):
                    acc[cell, i * PAD + RING : (i + 1) * PAD, :] = f
            return carry

        lax.fori_loop(0, n // span - 1, early, 0)
    inject(n - span + 1, True)

    def stitch(low, high):
        lane = lax.broadcasted_iota(jnp.int32, low.shape, 1)
        up = jnp.where(lane < depth - 1, pltpu.roll(low, depth - 1, 1), 0.0)
        down = jnp.where(lane > 0, pltpu.roll(high, 1, 1), 0.0)
        return low + down, high + up

    def join(a, ra, b, rb, size):
        total = acc[a, ra : ra + size, :] + acc[b, rb : rb + size, :]
        acc[a, ra : ra + size, :] = total
        acc[b, rb : rb + size, :] = total

    moves = moves_of(cx, cy)

    def there(m):
        return neighbour(m, gx, gy, nx, ny, cx, cy)

    def strip_copy(c, m, sem, mine, theirs):
        src, dst = ((xs, rx), (ys, ry), (cs, rc))[(m >= 2) + (m >= 4)]
        dx, dy = moves[m]
        return pltpu.make_async_remote_copy(
            src_ref=src.at[(c,) + mine],
            dst_ref=dst.at[(c,) + theirs],
            send_sem=halo_send.at[c * 8 + m],
            recv_sem=halo_recv.at[c * 8 + sem],
            device_id=(gx + dx, gy + dy),
            device_id_type=MESH,
        )

    def place(m):
        return (m % 2,) if m < 4 else ((m - 4) // 2, m % 2)

    def outgoing(c, m):
        return strip_copy(c, m, m, place(m), place(OPPOSITE[m]))

    def incoming(c, m):
        return strip_copy(c, m, OPPOSITE[m], place(m), place(m))

    for c in range(3):
        o = c * PAD
        for cell in range(cells):
            low, high = stitch(acc[cell, o : o + 16, :], acc[cell, o + 64 : o + 80, :])
            acc[cell, o : o + 16, :] = low
            acc[cell, o + 64 : o + 80, :] = high
        for r in range(5):
            k = o + r * 16
            for y in range(cy):
                for x in range(cx - 1):
                    join(x * cy + y, k + 8, (x + 1) * cy + y, k, 5)
            for x in range(cx):
                for y in range(cy - 1):
                    a, b = x * cy + y, x * cy + y + 1
                    join(a, k + 13, b, k + 5, 3)
                    join(a, k + 4, b, k, 1)
                    join(a, k + 12, b, k + 8, 1)
        for x in range(cx):
            for side in (0, 1):
                cell = x * cy + side * (cy - 1)
                for h in range(halves):
                    lanes = slice(h * 128, (h + 1) * 128)
                    for r in range(5):
                        k = o + r * 16
                        low, mid, high = ((0, 5, 8), (4, 13, 12))[side]
                        to = x * 25 * halves + r * halves + h
                        step = 5 * halves
                        ys[c, side, to : to + 1, :] = acc[cell, k + low : k + low + 1, lanes]
                        ys[c, side, pl.ds(to + step, 3, stride=step), :] = acc[
                            cell, k + mid : k + mid + 3, lanes
                        ]
                        ys[c, side, to + 4 * step : to + 4 * step + 1, :] = acc[
                            cell, k + high : k + high + 1, lanes
                        ]
        for m in (2, 3):
            @pl.when(there(m))
            def _():
                outgoing(c, m).start()
        for y in range(cy):
            for side in (0, 1):
                cell = side * (cx - 1) * cy + y
                for h in range(halves):
                    for r in range(5):
                        k = o + r * 16 + side * 8
                        xs[c, side, pl.ds(r * rows_node + h * cy + y, 5, stride=5 * rows_node), :] = (
                            acc[cell, k : k + 5, h * 128 : (h + 1) * 128]
                        )
        for x in (0, 1):
            for y in (0, 1):
                cell = x * (cx - 1) * cy + y * (cy - 1)
                for h in range(halves):
                    for r in range(5):
                        k = o + r * 16 + x * 8 + y * 4
                        cs[c, x, y, r * halves + h : r * halves + h + 1, :] = acc[
                            cell, k : k + 1, h * 128 : (h + 1) * 128
                        ]
        for m in (0, 1, 4, 5, 6, 7):
            @pl.when(there(m))
            def _():
                outgoing(c, m).start()

    def place_rows(cell, c, values, row, size, node, step):
        start = ((cell // cy) * 3 + c) * 125 * rows_node + cell % cy
        for h in range(halves):
            at = start + h * cy + node * rows_node
            part = values[row : row + size, h * 128 : (h + 1) * 128]
            pre[pl.ds(at, size, stride=step * rows_node), :] = part

    stores = []
    done = 0
    for x in range(cx):
        for y in range(cy):
            cell = x * cy + y
            inner = gather_core(cell)
            for c in range(3):
                f = inner[c]
                low, high = stitch(f[0:8], f[32:40])
                lane = lax.broadcasted_iota(jnp.int32, (8, depth), 1)
                row = lax.broadcasted_iota(jnp.int32, (8, depth), 0)
                tail = f[40:48]
                up = pltpu.roll(pltpu.roll(tail, depth - 1, 1), 4, 0)
                down = pltpu.roll(pltpu.roll(tail, 1, 1), 4, 0)
                tail = (
                    tail
                    + jnp.where((row == 4) & (lane < depth - 1), up, 0.0)
                    + jnp.where((row == 0) & (lane > 0), down, 0.0)
                )
                planes = [low, f[8:16], f[16:24], f[24:32], high]
                for r in range(5):
                    ring = acc[cell, c * PAD + r * 16 : c * PAD + r * 16 + 16, :]
                    place_rows(cell, c, ring, 0, 5, r, 5)
                    place_rows(cell, c, ring, 5, 3, 25 + r, 25)
                    place_rows(cell, c, ring, 8, 5, 100 + r, 5)
                    place_rows(cell, c, ring, 13, 3, 45 + r, 25)
                    place_rows(cell, c, planes[r], 0, 3, 30 + r, 5)
                    place_rows(cell, c, planes[r], 3, 3, 55 + r, 5)
                    place_rows(cell, c, planes[r], 6, 2, 80 + r, 5)
                place_rows(cell, c, tail, 0, 5, 90, 1)
        for c in range(3):
            upto = (x * 3 + c + 1) * 125 * rows_node // 8 * 8
            copy = pltpu.make_async_copy(
                pre.at[pl.ds(done, upto - done)],
                pre_h.at[pl.ds(done, upto - done)],
                store_sem.at[x * 3 + c],
            )
            copy.start()
            stores.append(copy)
            done = upto

    def drain(k, c):
        tile_copy(k, lax.rem(me + k, n), me).wait_send()
        return c

    lax.fori_loop(1, n, drain, 0)
    for c in range(3):
        for m in range(8):
            @pl.when(there(m))
            def _():
                incoming(c, m).wait_recv()
                outgoing(c, m).wait_send()
    for copy in stores:
        copy.wait()


def finish_kernel(
    nx, ny, cx, cy, pre_h, rx_h, ry_h, rc_h, out_h, buf, bx, by, bc, load_sem, strip_sem, out_sem
):
    gx, gy = lax.axis_index("gx"), lax.axis_index("gy")
    total = buf.shape[0]
    block = total // (cx * 3)
    rows_node = block // 125
    halves = rows_node // cy

    def strip(m):
        src, dst = ((rx_h, bx), (ry_h, by), (rc_h, bc))[(m >= 2) + (m >= 4)]
        at = (m % 2,) if m < 4 else ((m - 4) // 2, m % 2)
        where = (slice(None),) + at
        return pltpu.make_async_copy(src.at[where], dst.at[where], strip_sem.at[m]), dst, where

    def there(m):
        return neighbour(m, gx, gy, nx, ny, cx, cy)

    for m in range(8):
        copy, dst, where = strip(m)

        @pl.when(there(m))
        def _():
            copy.start()

        @pl.when(jnp.logical_not(there(m)))
        def _():
            hole = dst.at[where]
            hole[...] = jnp.zeros(hole.shape, F32)

    loads, done = [], 0
    for k in range(cx * 3):
        upto = min(-(-(k + 1) * block // 8) * 8, total)
        copy = pltpu.make_async_copy(
            pre_h.at[pl.ds(done, upto - done)], buf.at[pl.ds(done, upto - done)], load_sem.at[k]
        )
        copy.start()
        loads.append(copy)
        done = upto
    for m in range(8):
        copy, dst, where = strip(m)

        @pl.when(there(m))
        def _():
            copy.wait()

    stores, done = [], 0
    for k in range(cx * 3):
        x, c = k // 3, k % 3
        loads[k].wait()
        base = k * block
        face = 25 * rows_node
        if x == 0:
            buf[base : base + face, :] += bx[c, 0]
        if x == cx - 1:
            buf[base + 4 * face : base + 5 * face, :] += bx[c, 1]
        line = 5 * halves
        for side in (0, 1):
            y = side * (cy - 1)
            for p in range(5):
                at = base + (p * 25 + side * 20) * rows_node + y
                where = pl.ds(at, line, stride=cy)
                k0 = (x * 5 + p) * line
                add = by[c, side, k0 : k0 + line, :]
                if x == 0 and p == 0:
                    add = add + bc[c, 0, side]
                if x == cx - 1 and p == 4:
                    add = add + bc[c, 1, side]
                buf[where, :] += add
        upto = (k + 1) * block // 8 * 8
        copy = pltpu.make_async_copy(
            buf.at[pl.ds(done, upto - done)], out_h.at[pl.ds(done, upto - done)], out_sem.at[k]
        )
        copy.start()
        stores.append(copy)
        done = upto
    for copy in stores:
        copy.wait()


def anywhere(count):
    return [pl.BlockSpec(memory_space=pl.ANY)] * count


def body(nx, ny, wavefield, moduli, residuals, coords, angles, element_ids, counts):
    cx, cy, depth = wavefield.shape[0], wavefield.shape[1], wavefield.shape[4]
    n, slots = nx * ny, residuals.shape[2]
    cells, halves = cx * cy, depth // 128
    span = min(n, SPAN)
    width = TILES * slots
    rows = wavefield.transpose(0, 2, 3, 1, 4).reshape(cx, 3, 125, cy, halves, 128)
    rows = rows.transpose(0, 1, 2, 4, 3, 5).reshape(-1, 128)
    coords = coords.transpose(0, 2, 1, 3)
    moduli = moduli.reshape(cells, 2, depth)
    operands = [residuals, coords, angles, element_ids, counts, rows, moduli, *tables()]
    strips = [
        (3, 2, 25 * halves * cy, 128),
        (3, 2, cx * 25 * halves, 128),
        (3, 2, 2, 5 * halves, 128),
    ]
    scratch = [pltpu.VMEM(a.shape, a.dtype) for a in operands]
    scratch += [
        pltpu.VMEM(rows.shape, F32),
        pltpu.VMEM((n, 8, slots), F32),
        pltpu.VMEM((n, 8, slots), F32),
        pltpu.VMEM((cells, 3 * PAD, depth), F32),
        pltpu.VMEM((6 * RING, width), BF16),
        pltpu.VMEM((6 * RING, width), BF16),
        pltpu.VMEM((6 * CORE, span * slots // 2), BF16),
        pltpu.VMEM((6 * CORE, span * slots // 2), BF16),
        pltpu.VMEM((span * slots // 2, cells * depth), BF16),
        pltpu.VMEM((span * slots // 2, cells * depth), BF16),
        pltpu.VMEM((2, 3, PAD, depth), F32),
    ]
    scratch += [pltpu.VMEM(s, F32) for s in strips]
    scratch += [
        pltpu.SemaphoreType.DMA((len(operands),)),
        pltpu.SemaphoreType.DMA((cx * 3,)),
        pltpu.SemaphoreType.DMA((n,)),
        pltpu.SemaphoreType.DMA((n,)),
        pltpu.SemaphoreType.DMA((24,)),
        pltpu.SemaphoreType.DMA((24,)),
    ]
    parts = pl.pallas_call(
        functools.partial(step_kernel, nx, ny, cx, cy),
        out_shape=[jax.ShapeDtypeStruct(s, F32) for s in [rows.shape] + strips],
        in_specs=anywhere(len(operands)),
        out_specs=anywhere(4),
        scratch_shapes=scratch,
        compiler_params=pltpu.CompilerParams(collective_id=0, has_side_effects=True),
    )(*operands)
    force = pl.pallas_call(
        functools.partial(finish_kernel, nx, ny, cx, cy),
        out_shape=jax.ShapeDtypeStruct(rows.shape, F32),
        in_specs=anywhere(4),
        out_specs=anywhere(1)[0],
        scratch_shapes=[pltpu.VMEM(s, F32) for s in [rows.shape] + strips]
        + [
            pltpu.SemaphoreType.DMA((cx * 3,)),
            pltpu.SemaphoreType.DMA((8,)),
            pltpu.SemaphoreType.DMA((cx * 3,)),
        ],
    )(*parts)
    force = force.reshape(cx, 3, 125, halves, cy, 128).transpose(0, 1, 2, 4, 3, 5)
    return force.reshape(cx, 3, 125, cy, depth).transpose(0, 3, 1, 2, 4)


def solution(mesh):
    in_specs = (
        P("gx", "gy", None, None, None),
        P("gx", "gy", None, None),
        P(("gx", "gy"), None, None),
        P(("gx", "gy"), None, None, None),
        P(("gx", "gy"), None, None, None),
        P(("gx", "gy"), None, None),
        P(("gx", "gy"), None),
    )
    out_specs = P("gx", "gy", None, None, None)
    return jax.shard_map(
        functools.partial(body, mesh.shape["gx"], mesh.shape["gy"]),
        mesh=mesh,
        in_specs=in_specs,
        out_specs=out_specs,
        check_vma=False,
    )
```

time: 42.2 us -> 29.9 us (0.71)
  Pallas kernels: 39 us -> 29.7 us
  local copies, waits for them, and re-layouts: 3.05 us -> 0 us
    pallas_call x1, Pallas kernels: 39 us -> 27.2 us  [body(): pl.pallas_call(functools.partial(step_kernel, nx, ny, cx, cy), out_shape=...]
    unnamed x1 -> x0, local copies, waits for them, and re-layouts: 3.05 us -> none
    pallas_call x0 -> x1, Pallas kernels: none -> 2.5 us  [body(): pl.pallas_call(functools.partial(finish_kernel, nx, ny, cx, cy), out_shap...]
where the time goes in v1:
time: 29.9 us; the launch traced here: 29.7 us
  Pallas kernels  29.7 us (99%)
    pallas_call x1, Pallas kernels, body(): pl.pallas_call(functools.partial(step_kernel, nx, ny, cx, cy), out_shape=...  27.2 us
    pallas_call x1, Pallas kernels, body(): pl.pallas_call(functools.partial(finish_kernel, nx, ny, cx, cy), out_shap...  2.5 us

profile of v1, /device:TPU:0, one launch (start us, length us, event | category | flops | bytes accessed | tf_op | source)
XLA Modules:
  0.0 29.7 jit_solution(14747351047176577982)
XLA Ops:
  0.0 27.2 %shard_map.109 = (f32[3000,128]{1,0:T(8,128)}, f32[3,2,100,128]{3,2,1,0:T(8,128)}, f32[3,2,100,128]{3,2,1,0:T(8,128)}, f32[3,2,2,10,128]{4,3,2,1,0:T(8,128)}) custom-call(f32[1,32,128]{2,1,0:T(8,128)} %resid_h.1, f32[1,3,32,128]{3,2,1,0:T(8,128)} %bitcast.17, f32[1,32,2,128]{3,2,1,0:T(2,128)} %angle_h.1, s32[1,32,128]{2,1,0:T(8,128)} %ids_h.1, ...), custom_call_target="tpu_custom_call" | custom-call | tf_op jit(solution)/shard_map/pallas_call | solution.py:637
  27.2 2.5 %shard_map.110 = f32[3000,128]{1,0:T(8,128)} custom-call(f32[3000,128]{1,0:T(8,128)} %get-tuple-element.9.pre_h, f32[3,2,100,128]{3,2,1,0:T(8,128)} %get-tuple-element.10.rx_h, f32[3,2,100,128]{3,2,1,0:T(8,128)} %get-tuple-element.11.ry_h, f32[3,2,2,10,128]{4,3,2,1,0:T(8,128)} %get-tuple-element.12.rc_h), custom_call_target="tpu_custom_call" | custom-call | tf_op jit(solution)/shard_map/pallas_call | solution.py:645

commit v2 on v1

--- a/solution.py
+++ b/solution.py
@@ -136,30 +136,21 @@
     return ab * cd, (a + b) * cd + ab * (c + d)
 
 
-def moves_of(cx, cy):
-    moves = [(2 * s - 1, 0) for s in (0, 1)] + [(0, 2 * s - 1) for s in (0, 1)]
-    moves += [(2 * x - 1, 2 * y - 1) for x in (0, 1) for y in (0, 1)]
-    return moves
-
-
-OPPOSITE = [1, 0, 3, 2, 7, 6, 5, 4]
-
-
-def neighbour(m, gx, gy, nx, ny, cx, cy):
-    ok = None
-    for pos, step, total in ((gx, moves_of(cx, cy)[m][0], nx), (gy, moves_of(cx, cy)[m][1], ny)):
-        if step:
-            c = pos > 0 if step < 0 else pos < total - 1
-            ok = c if ok is None else ok & c
-    return ok
+MOVES = [(-1, 0), (1, 0), (0, -1), (0, 1)]
+
+
+def neighbour(m, gx, gy, nx, ny):
+    step = MOVES[m][m // 2]
+    pos, total = ((gx, nx), (gy, ny))[m // 2]
+    return pos > 0 if step < 0 else pos < total - 1
 
 
 def step_kernel(
     nx, ny, cx, cy, resid_h, coord_h, angle_h, ids_h, count_h, u_h, mod_h, g1_h, g2_h, bs_h,
-    consts_h, pre_h, rx, ry, rc,
-    resid, coord, angle, ids, count, u_ref, mod_ref, g1, g2, bs, consts, pre,
-    packed, got, acc, lhs_a, lhs_b, in_a, in_b, hot_a, hot_b, pad, xs, ys, cs,
-    load_sem, store_sem, send_sem, recv_sem, halo_send, halo_recv,
+    consts_h, pre_h, rx, ry, re,
+    resid, coord, angle, ids, count, u_ref, mod_ref, g1, g2, bs, consts,
+    packed, got, acc, lhs_a, lhs_b, in_a, in_b, hot_a, hot_b, pad, xs, ys, es, tips,
+    load_sem, send_sem, recv_sem, halo_send, halo_recv,
 ):
     n = nx * ny
     gx, gy = lax.axis_index("gx"), lax.axis_index("gy")
@@ -204,6 +195,13 @@
     packed[:, 5, :] = sa * cd
     packed[:, 6, :] = sd
     packed[:, 7, :] = ids[0].astype(F32)
+    tips[...] = jnp.zeros_like(tips)
+    for m in range(4):
+        @pl.when(jnp.logical_not(neighbour(m, gx, gy, nx, ny)))
+        def _():
+            for hole in ((rx,), (ry, re))[m // 2]:
+                hole[m % 2] = jnp.zeros(hole.shape[1:], F32)
+
     pl.semaphore_wait(barrier, n - 1)
 
     def tile_copy(k, to, at):
@@ -361,31 +359,45 @@
         acc[a, ra : ra + size, :] = total
         acc[b, rb : rb + size, :] = total
 
-    moves = moves_of(cx, cy)
-
     def there(m):
-        return neighbour(m, gx, gy, nx, ny, cx, cy)
-
-    def strip_copy(c, m, sem, mine, theirs):
-        src, dst = ((xs, rx), (ys, ry), (cs, rc))[(m >= 2) + (m >= 4)]
-        dx, dy = moves[m]
+        return neighbour(m, gx, gy, nx, ny)
+
+    quad = 4 * halves
+    line = (4 * cx - 1) * quad
+    last = slice(depth - 128, depth)
+
+    def strip_copy(src, dst, m, slot, where):
+        dx, dy = MOVES[m]
+        side, other = m % 2, 1 - m % 2
         return pltpu.make_async_remote_copy(
-            src_ref=src.at[(c,) + mine],
-            dst_ref=dst.at[(c,) + theirs],
-            send_sem=halo_send.at[c * 8 + m],
-            recv_sem=halo_recv.at[c * 8 + sem],
+            src_ref=src.at[(side,) + where],
+            dst_ref=dst.at[(other,) + where],
+            send_sem=halo_send.at[slot, m],
+            recv_sem=halo_recv.at[slot, m],
             device_id=(gx + dx, gy + dy),
             device_id_type=MESH,
         )
 
-    def place(m):
-        return (m % 2,) if m < 4 else ((m - 4) // 2, m % 2)
-
-    def outgoing(c, m):
-        return strip_copy(c, m, m, place(m), place(OPPOSITE[m]))
-
-    def incoming(c, m):
-        return strip_copy(c, m, OPPOSITE[m], place(m), place(m))
+    def arriving(src, dst, m, slot, where):
+        dx, dy = MOVES[m]
+        return pltpu.make_async_remote_copy(
+            src_ref=src.at[(m % 2,) + where],
+            dst_ref=dst.at[(m % 2,) + where],
+            send_sem=halo_send.at[slot, m],
+            recv_sem=halo_recv.at[slot, m + 1 - 2 * (m % 2)],
+            device_id=(gx + dx, gy + dy),
+            device_id_type=MESH,
+        )
+
+    def part(c):
+        return (pl.ds(c * line, line + (quad if c == 2 else 0)),)
+
+    def pack_tips(rows):
+        lane = lax.broadcasted_iota(jnp.int32, rows[0].shape, 1)
+        total = rows[0]
+        for c in (1, 2):
+            total = jnp.where(lane == 127 - c, pltpu.roll(rows[c], 128 - c, 1), total)
+        return total
 
     for c in range(3):
         o = c * PAD
@@ -404,59 +416,63 @@
                     join(a, k + 13, b, k + 5, 3)
                     join(a, k + 4, b, k, 1)
                     join(a, k + 12, b, k + 8, 1)
-        for x in range(cx):
-            for side in (0, 1):
+        for side in (0, 1):
+            low, mid, high = ((0, 5, 8), (4, 13, 12))[side]
+            for x in range(cx):
                 cell = x * cy + side * (cy - 1)
-                for h in range(halves):
-                    lanes = slice(h * 128, (h + 1) * 128)
-                    for r in range(5):
-                        k = o + r * 16
-                        low, mid, high = ((0, 5, 8), (4, 13, 12))[side]
-                        to = x * 25 * halves + r * halves + h
-                        step = 5 * halves
-                        ys[c, side, to : to + 1, :] = acc[cell, k + low : k + low + 1, lanes]
-                        ys[c, side, pl.ds(to + step, 3, stride=step), :] = acc[
+                for r in range(4):
+                    k = o + r * 16
+                    for h in range(halves):
+                        lanes = slice(h * 128, (h + 1) * 128)
+                        to = r * halves + h
+                        at = c * line + x * 4 * quad + to
+                        ys[side, pl.ds(at, 3, stride=quad), :] = acc[
                             cell, k + mid : k + mid + 3, lanes
                         ]
-                        ys[c, side, to + 4 * step : to + 4 * step + 1, :] = acc[
-                            cell, k + high : k + high + 1, lanes
-                        ]
+                        if x < cx - 1:
+                            ys[side, at + 3 * quad : at + 3 * quad + 1, :] = acc[
+                                cell, k + high : k + high + 1, lanes
+                            ]
+                        for e, row in ((0, low), (1, high)):
+                            if x == e * (cx - 1):
+                                at_e = (c * 2 + e) * quad + to
+                                es[side, at_e : at_e + 1, :] = acc[
+                                    cell, k + row : k + row + 1, lanes
+                                ]
+                k = o + 64
+                tips[side, c, x * 4 : x * 4 + 3, :] = acc[cell, k + mid : k + mid + 3, last]
+                for e, row in ((0, low), (1, high)):
+                    if x == e * (cx - 1):
+                        tips[2 + side, c, e : e + 1, :] = acc[cell, k + row : k + row + 1, last]
+                if x < cx - 1:
+                    tips[side, c, x * 4 + 3 : x * 4 + 4, :] = acc[cell, k + high : k + high + 1, last]
+            if c == 2:
+                ys[side, 3 * line : 3 * line + quad, :] = pack_tips([tips[side, d] for d in range(3)])
         for m in (2, 3):
             @pl.when(there(m))
             def _():
-                outgoing(c, m).start()
+                strip_copy(ys, ry, m, c, part(c)).start()
         for y in range(cy):
             for side in (0, 1):
                 cell = side * (cx - 1) * cy + y
                 for h in range(halves):
                     for r in range(5):
                         k = o + r * 16 + side * 8
-                        xs[c, side, pl.ds(r * rows_node + h * cy + y, 5, stride=5 * rows_node), :] = (
+                        xs[side, c, pl.ds(r * rows_node + h * cy + y, 5, stride=5 * rows_node), :] = (
                             acc[cell, k : k + 5, h * 128 : (h + 1) * 128]
                         )
-        for x in (0, 1):
-            for y in (0, 1):
-                cell = x * (cx - 1) * cy + y * (cy - 1)
-                for h in range(halves):
-                    for r in range(5):
-                        k = o + r * 16 + x * 8 + y * 4
-                        cs[c, x, y, r * halves + h : r * halves + h + 1, :] = acc[
-                            cell, k : k + 1, h * 128 : (h + 1) * 128
-                        ]
-        for m in (0, 1, 4, 5, 6, 7):
+        for m in (0, 1):
             @pl.when(there(m))
             def _():
-                outgoing(c, m).start()
+                strip_copy(xs, rx, m, c, (c,)).start()
 
     def place_rows(cell, c, values, row, size, node, step):
         start = ((cell // cy) * 3 + c) * 125 * rows_node + cell % cy
         for h in range(halves):
             at = start + h * cy + node * rows_node
             part = values[row : row + size, h * 128 : (h + 1) * 128]
-            pre[pl.ds(at, size, stride=step * rows_node), :] = part
-
-    stores = []
-    done = 0
+            pre_h[pl.ds(at, size, stride=step * rows_node), :] = part
+
     for x in range(cx):
         for y in range(cy):
             cell = x * cy + y
@@ -485,109 +501,93 @@
                     place_rows(cell, c, planes[r], 3, 3, 55 + r, 5)
                     place_rows(cell, c, planes[r], 6, 2, 80 + r, 5)
                 place_rows(cell, c, tail, 0, 5, 90, 1)
-        for c in range(3):
-            upto = (x * 3 + c + 1) * 125 * rows_node // 8 * 8
-            copy = pltpu.make_async_copy(
-                pre.at[pl.ds(done, upto - done)],
-                pre_h.at[pl.ds(done, upto - done)],
-                store_sem.at[x * 3 + c],
-            )
-            copy.start()
-            stores.append(copy)
-            done = upto
+
+    for m in (0, 1):
+        @pl.when(there(m))
+        def _():
+            for c in range(3):
+                arriving(xs, rx, m, c, (c,)).wait_recv()
+            for c in range(3):
+                for side in (0, 1):
+                    at = side * (20 * rows_node + cy - 1)
+                    k = (c * 2 + m) * quad
+                    es[side, k : k + quad, :] += rx[m, c, pl.ds(at, quad, stride=cy), :]
+                    tip = at + 4 * rows_node + (halves - 1) * cy
+                    tips[2 + side, c, m : m + 1, :] += rx[m, c, tip : tip + 1, :]
+
+    for side in (0, 1):
+        es[side, 6 * quad : 7 * quad, :] = pack_tips([tips[2 + side, d] for d in range(3)])
+        m = 2 + side
+
+        @pl.when(there(m))
+        def _():
+            strip_copy(es, re, m, 3, ()).start()
 
     def drain(k, c):
         tile_copy(k, lax.rem(me + k, n), me).wait_send()
         return c
 
     lax.fori_loop(1, n, drain, 0)
-    for c in range(3):
-        for m in range(8):
-            @pl.when(there(m))
-            def _():
-                incoming(c, m).wait_recv()
-                outgoing(c, m).wait_send()
-    for copy in stores:
-        copy.wait()
-
-
-def finish_kernel(
-    nx, ny, cx, cy, pre_h, rx_h, ry_h, rc_h, out_h, buf, bx, by, bc, load_sem, strip_sem, out_sem
-):
-    gx, gy = lax.axis_index("gx"), lax.axis_index("gy")
+    for m in (0, 1):
+        @pl.when(there(m))
+        def _():
+            for c in range(3):
+                strip_copy(xs, rx, m, c, (c,)).wait_send()
+
+    for m in (2, 3):
+        @pl.when(there(m))
+        def _():
+            for c in range(3):
+                arriving(ys, ry, m, c, part(c)).wait_recv()
+                strip_copy(ys, ry, m, c, part(c)).wait_send()
+            arriving(es, re, m, 3, ()).wait_recv()
+            strip_copy(es, re, m, 3, ()).wait_send()
+
+
+def finish_kernel(cx, cy, pre, rx, ry, re, out_h, buf, out_sem):
     total = buf.shape[0]
     block = total // (cx * 3)
     rows_node = block // 125
     halves = rows_node // cy
-
-    def strip(m):
-        src, dst = ((rx_h, bx), (ry_h, by), (rc_h, bc))[(m >= 2) + (m >= 4)]
-        at = (m % 2,) if m < 4 else ((m - 4) // 2, m % 2)
-        where = (slice(None),) + at
-        return pltpu.make_async_copy(src.at[where], dst.at[where], strip_sem.at[m]), dst, where
-
-    def there(m):
-        return neighbour(m, gx, gy, nx, ny, cx, cy)
-
-    for m in range(8):
-        copy, dst, where = strip(m)
-
-        @pl.when(there(m))
-        def _():
-            copy.start()
-
-        @pl.when(jnp.logical_not(there(m)))
-        def _():
-            hole = dst.at[where]
-            hole[...] = jnp.zeros(hole.shape, F32)
-
-    loads, done = [], 0
-    for k in range(cx * 3):
-        upto = min(-(-(k + 1) * block // 8) * 8, total)
-        copy = pltpu.make_async_copy(
-            pre_h.at[pl.ds(done, upto - done)], buf.at[pl.ds(done, upto - done)], load_sem.at[k]
-        )
-        copy.start()
-        loads.append(copy)
-        done = upto
-    for m in range(8):
-        copy, dst, where = strip(m)
-
-        @pl.when(there(m))
-        def _():
-            copy.wait()
-
-    stores, done = [], 0
+    plane, quad = 25 * rows_node, 4 * halves
+    line = (4 * cx - 1) * quad
+    lane = lax.broadcasted_iota(jnp.int32, (quad, 128), 1)
+    row = lax.broadcasted_iota(jnp.int32, (quad, 128), 0)
+    copies, done = [], 0
     for k in range(cx * 3):
         x, c = k // 3, k % 3
-        loads[k].wait()
         base = k * block
-        face = 25 * rows_node
+        buf[base : base + block, :] = pre[base : base + block, :]
         if x == 0:
-            buf[base : base + face, :] += bx[c, 0]
+            buf[base : base + plane, :] += rx[0, c]
         if x == cx - 1:
-            buf[base + 4 * face : base + 5 * face, :] += bx[c, 1]
-        line = 5 * halves
+            buf[base + 4 * plane : base + 5 * plane, :] += rx[1, c]
         for side in (0, 1):
-            y = side * (cy - 1)
+            tips = pltpu.roll(ry[side, 3 * line : 3 * line + quad, :], c, 1)
+            ends = pltpu.roll(re[side, 6 * quad : 7 * quad, :], c, 1)
             for p in range(5):
-                at = base + (p * 25 + side * 20) * rows_node + y
-                where = pl.ds(at, line, stride=cy)
-                k0 = (x * 5 + p) * line
-                add = by[c, side, k0 : k0 + line, :]
-                if x == 0 and p == 0:
-                    add = add + bc[c, 0, side]
-                if x == cx - 1 and p == 4:
-                    add = add + bc[c, 1, side]
-                buf[where, :] += add
+                pp = x * 4 + p
+                if pp % (4 * cx) == 0:
+                    e = pp // (4 * cx)
+                    at = (c * 2 + e) * quad
+                    values, tip = re[side, at : at + quad, :], ends[e : e + 1]
+                else:
+                    at = c * line + (pp - 1) * quad
+                    values, tip = ry[side, at : at + quad, :], tips[pp - 1 : pp]
+                ahead = pltpu.roll(values, 127, 1)
+                beyond = jnp.where(row == halves - 1, tip, pltpu.roll(ahead, quad - 1, 0))
+                upper = jnp.where(lane < 127, ahead, beyond)
+                to = base + (p * 25 + side * 20) * rows_node + side * (cy - 1)
+                buf[pl.ds(to, quad, stride=cy), :] += values
+                buf[pl.ds(to + quad * cy, halves, stride=cy), :] += upper[:halves]
         upto = (k + 1) * block // 8 * 8
         copy = pltpu.make_async_copy(
             buf.at[pl.ds(done, upto - done)], out_h.at[pl.ds(done, upto - done)], out_sem.at[k]
         )
         copy.start()
-        stores.append(copy)
+        copies.append(copy)
         done = upto
-    for copy in stores:
+    for copy in copies:
         copy.wait()
 
 
@@ -606,14 +606,14 @@
     coords = coords.transpose(0, 2, 1, 3)
     moduli = moduli.reshape(cells, 2, depth)
     operands = [residuals, coords, angles, element_ids, counts, rows, moduli, *tables()]
-    strips = [
-        (3, 2, 25 * halves * cy, 128),
-        (3, 2, cx * 25 * halves, 128),
-        (3, 2, 2, 5 * halves, 128),
+    quad = 4 * halves
+    received = [
+        (2, 3, 25 * halves * cy, 128),
+        (2, 3 * (4 * cx - 1) * quad + quad, 128),
+        (2, 7 * quad, 128),
     ]
     scratch = [pltpu.VMEM(a.shape, a.dtype) for a in operands]
     scratch += [
-        pltpu.VMEM(rows.shape, F32),
         pltpu.VMEM((n, 8, slots), F32),
         pltpu.VMEM((n, 8, slots), F32),
         pltpu.VMEM((cells, 3 * PAD, depth), F32),
@@ -625,34 +625,29 @@
         pltpu.VMEM((span * slots // 2, cells * depth), BF16),
         pltpu.VMEM((2, 3, PAD, depth), F32),
     ]
-    scratch += [pltpu.VMEM(s, F32) for s in strips]
+    scratch += [pltpu.VMEM(s, F32) for s in received + [(4, 3, quad, 128)]]
     scratch += [
         pltpu.SemaphoreType.DMA((len(operands),)),
-        pltpu.SemaphoreType.DMA((cx * 3,)),
         pltpu.SemaphoreType.DMA((n,)),
         pltpu.SemaphoreType.DMA((n,)),
-        pltpu.SemaphoreType.DMA((24,)),
-        pltpu.SemaphoreType.DMA((24,)),
+        pltpu.SemaphoreType.DMA((4, 4)),
+        pltpu.SemaphoreType.DMA((4, 4)),
     ]
     parts = pl.pallas_call(
         functools.partial(step_kernel, nx, ny, cx, cy),
-        out_shape=[jax.ShapeDtypeStruct(s, F32) for s in [rows.shape] + strips],
+        out_shape=[pltpu.VMEM(s, F32) for s in [rows.shape] + received],
         in_specs=anywhere(len(operands)),
-        out_specs=anywhere(4),
+        out_specs=[pl.BlockSpec(memory_space=pltpu.VMEM)] * 4,
         scratch_shapes=scratch,
-        compiler_params=pltpu.CompilerParams(collective_id=0, has_side_effects=True),
-    )(*operands)
+        compiler_params=pltpu.CompilerParams(collective_id=0, has_side_effects=True, vmem_limit_bytes=48 << 20),
+    )(*[pltpu.with_memory_space_constraint(a, pltpu.HBM) for a in operands])
     force = pl.pallas_call(
-        functools.partial(finish_kernel, nx, ny, cx, cy),
+        functools.partial(finish_kernel, cx, cy),
         out_shape=jax.ShapeDtypeStruct(rows.shape, F32),
-        in_specs=anywhere(4),
+        in_specs=[pl.BlockSpec(memory_space=pltpu.VMEM)] * 4,
         out_specs=anywhere(1)[0],
-        scratch_shapes=[pltpu.VMEM(s, F32) for s in [rows.shape] + strips]
-        + [
-            pltpu.SemaphoreType.DMA((cx * 3,)),
-            pltpu.SemaphoreType.DMA((8,)),
-            pltpu.SemaphoreType.DMA((cx * 3,)),
-        ],
+        scratch_shapes=[pltpu.VMEM(rows.shape, F32), pltpu.SemaphoreType.DMA((cx * 3,))],
+        compiler_params=pltpu.CompilerParams(vmem_limit_bytes=16 << 20),
     )(*parts)
     force = force.reshape(cx, 3, 125, halves, cy, 128).transpose(0, 1, 2, 4, 3, 5)
     return force.reshape(cx, 3, 125, cy, depth).transpose(0, 3, 1, 2, 4)

time: 29.9 us -> 26 us (0.87)
  Pallas kernels: 29.7 us -> 25.9 us
    pallas_call x1, Pallas kernels: 27.2 us -> 24.6 us  [body(): pl.pallas_call(functools.partial(step_kernel, nx, ny, cx, cy), out_shape=...]
    pallas_call x1, Pallas kernels: 2.5 us -> 1.27 us  [body(): pl.pallas_call(functools.partial(finish_kernel, cx, cy), out_shape=jax.Sh...]
where the time goes in v2:
time: 26 us; the launch traced here: 25.9 us
  Pallas kernels  25.9 us (100%)
    pallas_call x1, Pallas kernels, body(): pl.pallas_call(functools.partial(step_kernel, nx, ny, cx, cy), out_shape=...  24.6 us
    pallas_call x1, Pallas kernels, body(): pl.pallas_call(functools.partial(finish_kernel, cx, cy), out_shape=jax.Sh...  1.27 us

profile of v2, /device:TPU:0, one launch (start us, length us, event | category | flops | bytes accessed | tf_op | source)
XLA Modules:
  0.0 25.9 jit_solution(16471399695860105280)
XLA Ops:
  0.0 24.6 %shard_map.109 = (f32[3000,128]{1,0:T(8,128)S(1)}, f32[2,3,100,128]{3,2,1,0:T(8,128)S(1)}, f32[2,176,128]{2,1,0:T(8,128)S(1)}, f32[2,56,128]{2,1,0:T(8,128)S(1)}) custom-call(f32[1,32,128]{2,1,0:T(8,128)} %resid_h.1, f32[1,3,32,128]{3,2,1,0:T(8,128)} %bitcast.17, f32[1,32,2,128]{3,2,1,0:T(2,128)} %angle_h.1, s32[1,32,128]{2,1,0:T(8,128)} %ids_h.1, ...), custom_call_target="tpu_custom_call" | custom-call | tf_op jit(solution)/shard_map/pallas_call | solution.py:636
  24.6 1.3 %shard_map.110 = f32[3000,128]{1,0:T(8,128)} custom-call(f32[3000,128]{1,0:T(8,128)S(1)} %get-tuple-element.9.pre, f32[2,3,100,128]{3,2,1,0:T(8,128)S(1)} %get-tuple-element.10.rx, f32[2,176,128]{2,1,0:T(8,128)S(1)} %get-tuple-element.11.ry, f32[2,56,128]{2,1,0:T(8,128)S(1)} %get-tuple-element.12.re), custom_call_target="tpu_custom_call" | custom-call | tf_op jit(solution)/shard_map/pallas_call | solution.py:644
